TPU v7x, 32 devices: a whole 2x2x4 slice. The times are simulated.
32 devices in a mesh: groups: 2 (over x), tok: 16 (over z, y, core).
Axes of the slice: x: 2, y: 2, z: 4, core: 2. Of those that a mesh axis runs over, the one named last changes fastest.
Arguments:
- activations: bfloat16 [32, 128, 768], P(('groups', 'tok')), parts along dimension 0, may hold values from -32 to 32
- pair_repr: bfloat16 [256, 128, 128], P('groups', 'tok'), parts along dimension 0, may hold values from -6 to 6
- pair_gain: float32 [128], replicated, may hold values from 0.5 to 1.5
- bias_weight: float32 [128, 16], replicated, may hold values from -0.5 to 0.5
- proj_weight: bfloat16 [768, 3072], replicated, may hold values from -0.21875 to 0.21875
- query_bias: float32 [768], replicated, may hold values from -5 to 5
- out_weight: bfloat16 [768, 768], replicated, may hold values from -0.21875 to 0.21875
- token_mask: int32 [256], P('groups'), parts along dimension 0, may hold values 0 or 1
- out_cotangent: bfloat16 [32, 128, 768], P(('groups', 'tok')), parts along dimension 0, may hold values from -6 to 6
Outputs:
- grad_activations: bfloat16 [32, 128, 768], P(('groups', 'tok')), parts along dimension 0
- grad_pair: bfloat16 [256, 128, 128], P('groups', 'tok'), parts along dimension 0
- grad_proj: float32 [1536, 3072], P(('groups', 'tok')), parts along dimension 0
- grad_out_weight: float32 [1536, 768], P(('groups', 'tok')), parts along dimension 0
- grad_query_bias: float32 [1536], P('groups'), parts along dimension 0
- grad_bias_weight: float32 [256, 16], P('groups'), parts along dimension 0
- grad_pair_gain: float32 [256], P('groups'), parts along dimension 0
There are 2 independent parts, one for each index of `groups`. A program takes and returns all parts, laid end to end along the dimension named above; an argument that names none is the same for every part. Nothing has to cross between parts.
All inputs are finite; a program needn't handle non-finite values.
Results may differ from a plain program's by a relative error of at most 0.015.
The roundings to bfloat16 on the way count: a program that leaves them out, or rounds other values in their place, can miss the bound.
Values may be sent and summed in bfloat16 or wider, within the bound.
A program may use at most 128 MiB of HBM per device.

v0:
```python
import math

import jax
import jax.numpy as jnp
from jax import lax
from jax.sharding import PartitionSpec as P

HEADS = 16
HD = 48


EPSILON = 1e-05
MASK_PENALTY = 10000.0


def as_sent(value):
    return jax.tree.map(lambda a: a.astype(jnp.bfloat16) if a.dtype == jnp.float32 else a, value)


def partner(block, axis, apart):
    count = lax.axis_size(axis)
    route = []
    for low in range(count):
        high = low | 1 << apart
        if high != low and high < count:
            route += [(low, high), (high, low)]
    return lax.ppermute(block, axis, route)


def dest_order(tensor):
    return tensor.reshape((tensor.shape[0] * tensor.shape[1],) + tensor.shape[2:])


def source_heads(tensor, blocks):
    rest = tensor.shape[1:]
    return tensor.reshape((HEADS, blocks) + rest)


def row_blocks(tensor, blocks):
    channels = tensor.shape[0]
    block_rows = tensor.shape[3] // blocks
    shaped = tensor.reshape(channels, HEADS, HD, blocks, block_rows)
    return dest_order(shaped.transpose(1, 3, 0, 2, 4))


def token_rows(tensor, blocks):
    shaped = source_heads(tensor, blocks)
    channels = shaped.shape[2]
    block_rows = shaped.shape[4]
    return shaped.transpose(1, 4, 2, 0, 3).reshape(blocks * block_rows, channels * HEADS * HD)


def grouped(tree, group_size):
    return tree.reshape((tree.shape[0] // group_size, group_size) + tree.shape[1:])


def ungrouped(tree):
    return tree.reshape((tree.shape[0] * tree.shape[1],) + tree.shape[2:])


def xor_order(array, position, bit_count):
    for level in range(bit_count):
        shaped = array.reshape((array.shape[0] // (2 << level), 2, 1 << level) + array.shape[1:])
        bit_set = position // (1 << level) % 2
        array = jnp.where(bit_set == 1, shaped[:, ::-1], shaped).reshape(array.shape)
    return array


def group_regroup(array, position, bit_count, offset):
    holding = xor_order(array, position, bit_count)
    for level in range(bit_count):
        shaped = holding.reshape(
            (holding.shape[0] // (2 << level), 2, 1 << level) + holding.shape[1:]
        )
        arrived_half = partner(as_sent(shaped[:, 1]), "tok", offset + level)
        holding = jnp.stack([shaped[:, 0], arrived_half], axis=1).reshape(holding.shape)
    return xor_order(holding, position, bit_count)


def probabilities(query, keys, bias_full, key_bias):
    scores = jnp.einsum("di,dj->ij", query, keys, preferred_element_type=jnp.float32) * HD ** (-0.5)
    scores = scores + bias_full + key_bias[None, :]
    peak = jnp.max(scores, axis=1, keepdims=True)
    expo = jnp.exp(scores - peak)
    return expo / jnp.sum(expo, axis=1, keepdims=True)


def attend_forward(values, probs):
    return jnp.einsum(
        "dj,ij->di", values, probs.astype(jnp.bfloat16), preferred_element_type=jnp.float32
    ).astype(jnp.bfloat16)


def gate_terms(grad_gated, gate, attended):
    gate32 = gate.astype(jnp.float32)
    grad32 = grad_gated.astype(jnp.float32)
    att32 = attended.astype(jnp.float32)
    gated = (gate32 * att32).astype(jnp.bfloat16)
    grad_att = (grad32 * gate32).astype(jnp.bfloat16)
    grad_logit = (grad32 * att32 * gate32 * (1.0 - gate32)).astype(jnp.bfloat16)
    return (grad_att, grad_logit, gated)


def attend_back(query, keys, values, probs, grad_att):
    rounded = probs.astype(jnp.bfloat16)
    grad_value = jnp.einsum("di,ij->dj", grad_att, rounded, preferred_element_type=jnp.float32)
    grad_probs = jnp.einsum("di,dj->ij", grad_att, values, preferred_element_type=jnp.float32)
    grad_scores = probs * (grad_probs - jnp.sum(probs * grad_probs, axis=1, keepdims=True))
    scores_b = grad_scores.astype(jnp.bfloat16)
    grad_query = jnp.einsum(
        "ij,dj->di", scores_b, keys, preferred_element_type=jnp.float32
    ) * HD ** (-0.5)
    grad_key = jnp.einsum(
        "ij,di->dj", scores_b, query, preferred_element_type=jnp.float32
    ) * HD ** (-0.5)
    return (grad_query.astype(jnp.bfloat16), jnp.stack([grad_key, grad_value], axis=0), grad_scores)


def make_joint(bias_full, key_bias):

    def joint_one(front, kv_one):
        probs = probabilities(front[0], kv_one[0], bias_full, key_bias)
        attended_one = attend_forward(kv_one[1], probs)
        grad_att, grad_logit, gated_one = gate_terms(front[2], front[1], attended_one)
        grad_query, grad_kv, grad_scores = attend_back(
            front[0], kv_one[0], kv_one[1], probs, grad_att
        )
        return (jnp.stack([grad_query, grad_logit, gated_one], axis=0), grad_kv, grad_scores)

    return joint_one


def on_device(
    activations,
    pair_repr,
    pair_gain,
    bias_weight,
    proj_weight,
    query_bias,
    out_weight,
    token_mask,
    out_cotangent,
):
    tok_count = lax.axis_size("tok")
    blocks = tok_count // HEADS
    all_tokens = activations.shape[1]
    feature = activations.shape[2]
    block_rows = all_tokens // blocks
    bit_count = blocks.bit_length() - 1
    position = lax.axis_index("tok") % blocks
    offset = 0
    act_rows = activations.reshape(all_tokens, feature)
    cot_rows = out_cotangent.reshape(all_tokens, feature)
    proj = jnp.dot(act_rows, proj_weight, preferred_element_type=jnp.float32)
    shift = jnp.concatenate([query_bias, jnp.zeros((2 * feature,), jnp.float32)])
    qkv_rows = (proj[:, : 3 * feature] + shift[None, :]).astype(jnp.bfloat16)
    gate = jax.nn.sigmoid(proj[:, 3 * feature :]).astype(jnp.bfloat16)
    grad_gated = jnp.einsum(
        "rn,mn->rm", cot_rows, out_weight, preferred_element_type=jnp.float32
    ).astype(jnp.bfloat16)
    pair_f = pair_repr.astype(jnp.float32)
    mean_z = jnp.mean(pair_f, axis=-1, keepdims=True)
    centred = pair_f - mean_z
    rstd = lax.rsqrt(jnp.mean(centred * centred, axis=-1, keepdims=True) + EPSILON)
    normed = centred * rstd
    scaled = normed * pair_gain
    bias_cols = jnp.einsum(
        "ijc,ch->hij", scaled, bias_weight, precision=lax.Precision.HIGHEST
    ).astype(jnp.bfloat16)
    key_bias = (token_mask.astype(jnp.float32) - 1.0) * MASK_PENALTY
    joint_rows = jnp.concatenate([qkv_rows[:, :feature], gate, grad_gated], axis=1)
    bias_wide = jnp.broadcast_to(bias_cols[:, None], (HEADS, blocks) + bias_cols.shape[1:])
    bias_full = lax.all_to_all(
        dest_order(bias_wide), "tok", split_axis=0, concat_axis=2, tiled=True
    )[0].astype(jnp.float32)
    per_item = make_joint(bias_full, key_bias)
    five_rows = jnp.concatenate([joint_rows, qkv_rows[:, feature:]], axis=1)
    five_view = five_rows.reshape(all_tokens, 5, HEADS, HD).transpose(1, 2, 3, 0)
    arrived = lax.all_to_all(
        row_blocks(five_view, blocks), "tok", split_axis=0, concat_axis=0, tiled=True
    )
    regrouped = group_regroup(
        arrived.reshape((blocks, HEADS) + arrived.shape[1:]), position, bit_count, offset
    )
    head_items = regrouped.transpose(1, 2, 3, 0, 4).reshape(HEADS, 5, HD, all_tokens)
    group_size = math.gcd(HEADS, max(1, 512 // all_tokens))

    def sample_step(total, pieces):
        merged, grad_kv, grad_scores = jax.vmap(per_item)(pieces[:, :3], pieces[:, 3:])
        results = jnp.concatenate([merged, grad_kv.astype(jnp.bfloat16)], axis=1)
        return (total + jnp.sum(grad_scores, axis=0), results)

    start_total = jnp.zeros((all_tokens, all_tokens), jnp.float32)
    grad_bias_part, results = lax.scan(sample_step, start_total, grouped(head_items, group_size))
    results = ungrouped(results)
    outgoing = results.reshape(HEADS, 5, HD, blocks, block_rows).transpose(3, 0, 1, 2, 4)
    returned = group_regroup(outgoing, position, bit_count, offset).reshape(
        tok_count, 5, HD, block_rows
    )
    came_back = lax.all_to_all(returned, "tok", split_axis=0, concat_axis=0, tiled=True)
    rows_back = token_rows(came_back, blocks)
    grad_rows = jnp.concatenate(
        [rows_back[:, :feature], rows_back[:, 3 * feature :], rows_back[:, feature : 2 * feature]],
        axis=1,
    )
    gated = rows_back[:, 2 * feature : 3 * feature]
    received = lax.all_to_all(
        grad_bias_part[None].astype(jnp.bfloat16), "tok", split_axis=2, concat_axis=0, tiled=True
    ).astype(jnp.float32)
    grad_bias = jnp.sum(source_heads(received, blocks), axis=1)
    first = jnp.einsum("rc,rn->cn", act_rows, grad_rows, preferred_element_type=jnp.float32)
    second = jnp.einsum("rc,rn->cn", gated, cot_rows, preferred_element_type=jnp.float32)
    weight_grads = lax.psum_scatter(
        jnp.concatenate([first, second], axis=1), "tok", scatter_dimension=0, tiled=True
    )
    grad_activations = jnp.einsum(
        "rn,dn->rd", grad_rows, proj_weight, preferred_element_type=jnp.float32
    ).astype(jnp.bfloat16)
    grad_zg = jnp.einsum("hij,ch->ijc", grad_bias, bias_weight, precision=lax.Precision.HIGHEST)
    weight_part = jnp.einsum("ijc,hij->ch", scaled, grad_bias, precision=lax.Precision.HIGHEST)
    gain_part = jnp.sum(normed * grad_zg, axis=(0, 1))
    query_part = jnp.sum(grad_rows[:, :feature].astype(jnp.float32), axis=0)
    grad_query_bias, grad_bias_weight, grad_pair_gain = lax.psum(
        (query_part, weight_part, gain_part), "tok"
    )
    grad_norm = grad_zg * pair_gain
    grad_pair = (
        grad_norm
        - jnp.mean(grad_norm, axis=-1, keepdims=True)
        - normed * jnp.mean(grad_norm * normed, axis=-1, keepdims=True)
    ) * rstd
    return (
        grad_activations.reshape(1, all_tokens, feature),
        grad_pair.astype(jnp.bfloat16),
        weight_grads[:, : 4 * feature],
        weight_grads[:, 4 * feature :],
        grad_query_bias,
        grad_bias_weight,
        grad_pair_gain,
    )


def solution(mesh):
    in_specs = (
        P(("groups", "tok"), None, None),
        P("groups", "tok", None),
        P(),
        P(),
        P(),
        P(),
        P(),
        P("groups"),
        P(("groups", "tok"), None, None),
    )
    out_specs = (
        P(("groups", "tok"), None, None),
        P("groups", "tok", None),
        P(("groups", "tok"), None),
        P(("groups", "tok"), None),
        P("groups"),
        P("groups", None),
        P("groups"),
    )
    return jax.shard_map(
        on_device, mesh=mesh, in_specs=in_specs, out_specs=out_specs, check_vma=False
    )
```

profile of v0, /device:TPU:0, one launch (start us, length us, event | category | flops | bytes accessed | tf_op | source)
XLA Modules:
  0.0 252.7 jit_solution(9659718730812204163)
XLA Ops:
  7.2 1.2 copy.67
  8.6 1.2 fusion.28
  10.4 7.4 %all-to-all-start.1 = ((bf16[16,128,8]{1,2,0:T(8,128)(2,1)}), bf16[16,128,8]{1,2,0:T(8,128)(2,1)S(1)}, u32[]{:S(2)}, u32[]{:S(2)}) async-start(bf16[16,128,8]{1,2,0:T(8,128)(2,1)} %copy.69), calls=%async_computation.1 | async-start | bytes 65536 | tf_op jit(solution)/shard_map/all_to_all | solution.py:173
  17.9 3.2 %fusion.58 = f32[128,3072]{1,0:T(8,128)S(1)} fusion(bf16[768,3072]{1,0:T(8,128)(2,1)} %param.15, bf16[1,128,768]{2,1,0:T(8,128)(2,1)} %param.11), kind=kOutput, calls=%fused_computation.93 | convolution fusion | flops 603979776 | bytes 6488064 | tf_op jit(solution)/shard_map/dot_general | solution.py:154
  23.3 1.0 copy.66
  24.5 5.9 %all-to-all-start = ((bf16[16,5,48,128]{3,2,1,0:T(8,128)(2,1)}), bf16[16,5,48,128]{3,2,1,0:T(8,128)(2,1)S(1)}, u32[]{:S(2)}, u32[]{:S(2)}) async-start(bf16[16,5,48,128]{3,2,1,0:T(8,128)(2,1)} %copy.66), calls=%async_computation | async-start | bytes 1966080 | tf_op jit(solution)/shard_map/all_to_all | solution.py:179
  30.5 21.7 %all-to-all-done = bf16[16,5,48,128]{3,2,1,0:T(8,128)(2,1)S(1)} async-done(((bf16[16,5,48,128]{3,2,1,0:T(8,128)(2,1)}), bf16[16,5,48,128]{3,2,1,0:T(8,128)(2,1)S(1)}, u32[]{:S(2)}, u32[]{:S(2)}) %all-to-all-start) | async-done | bytes 983072 | tf_op jit(solution)/shard_map/all_to_all | solution.py:179
  52.2 10.9 %while.13 = (s32[]{:T(128)}, f32[128,128]{0,1:T(8,128)S(1)}, bf16[4,4,5,48,128]{4,3,2,1,0:T(8,128)(2,1)}, bf16[4,4,5,48,128]{4,3,2,1,0:T(8,128)(2,1)S(1)}, f32[1...) while((s32[]{:T(128)}, f32[128,128]{0,1:T(8,128)S(1)}, ...), condition=%wide.region_7.8_spmd.clone, body=%wide.region_2.7_spmd.clone.sunk | while | flops 52896640 | bytes 4685423 | solution.py:194
  59.7 0.7 copy_dynamic-update-slice_fusion.2
  62.4 0.7 copy_dynamic-update-slice_fusion.2
  63.1 30.0 %all_to_all.34 = bf16[16,5,48,128]{3,2,1,0:T(8,128)(2,1)S(1)} all-to-all(bf16[16,5,48,128]{3,2,1,0:T(8,128)(2,1)} %bitcast.220), channel_id=1, replica_groups=mesh['groups'=2,'tok'=16] {'tok'}, dimensions={0} | all-to-all | bytes 1966080 | tf_op jit(solution)/shard_map/all_to_all | solution.py:200
  93.3 0.8 copy-done.2
  94.6 1.4 convolution_bitcast_fusion
  95.9 4.6 %pad_maximum_fusion = f32[768,3840]{0,1:T(8,128)} fusion(f32[768,768]{0,1:T(8,128)S(1)} %fusion.53, f32[768,3072]{0,1:T(8,128)S(1)} %convolution_bitcast_fusion), kind=kLoop, calls=%fused_computation.49 | loop fusion | flops 2949120 | bytes 23592960 | tf_op jit(solution)/shard_map/concatenate | solution.py:214
  100.6 12.4 %copy.86 = f32[768,3840]{1,0:T(8,128)} copy(f32[768,3840]{0,1:T(8,128)} %pad_maximum_fusion) | data formatting | bytes 23592960
  113.8 0.8 reduce
  114.6 11.2 %all_to_all.35 = bf16[16,2,512]{2,1,0:T(2,128)(2,1)S(1)} all-to-all(bf16[16,2,512]{2,1,0:T(2,128)(2,1)S(1)} %reshape.98), channel_id=1, replica_groups=mesh['groups'=2,'tok'=16] {'tok'}, dimensions={0} | all-to-all | bytes 65536 | tf_op jit(solution)/shard_map/all_to_all | solution.py:207
  126.7 0.9 copy.77
  127.6 1.2 convolution_bitcast_fusion.1
  129.0 60.7 %all-reduce.1 = (f32[768]{0:T(1024)}, f32[128,16]{0,1:T(8,128)}, f32[128]{0:T(128)}) all-reduce(f32[768]{0:T(1024)S(1)} %convert_reduce_fusion.1, f32[128,16]{0,1:T(8,128)S(1)} %convolution_bitcast_fusion.1, f32[128]{0:T(128)S(1)} %get-tuple-element.109), channel_id=1, replica_groups=mesh['groups'=2,'tok'=16] {'tok'}, use_global_device_ids=true, to_apply=%region_12.13 | all-reduce | flops 2944 | bytes 23552 | tf_op jit(solution)/shard_map/psum | solution.py:223
  189.7 4.7 %fusion.27 = bf16[1,128,768]{2,1,0:T(8,128)(2,1)} fusion(bf16[768,3072]{1,0:T(8,128)(2,1)} %param.15, bf16[128,768]{0,1:T(8,128)(2,1)S(1)} %get-tuple-element.136, bf16[128,1536]{0,1:T(8,128)(2,1)S(1)} %slice.80, bf16[128,768]{0,1:T(8,128)(2,1)S(1)} %get-tuple-element.135), kind=kOutput, calls=%fused_computation.55 | convolution fusion | flops 606437376 | bytes 5701632 | tf_op jit(solution)/shard_map/rn,dn->rd/dot_general | solution.py:216
  194.4 48.0 %reduce-scatter.4.cloned.1.call-done = f32[48,3840]{1,0:T(8,128)} async-done(((f32[768,3840]{1,0:T(8,128)}), f32[48,3840]{1,0:T(8,128)}) %reduce-scatter.4.cloned.1.call-update) | async-done | bytes 737296
  242.4 1.6 slice.84
  244.0 1.9 slice.83
  (97 shorter events, 14.7 us)
Async XLA Ops:
  7.2 14.2 %copy-start = (bf16[768,768]{1,0:T(8,128)(2,1)S(1)}, bf16[768,768]{1,0:T(8,128)(2,1)}, u32[]{:S(2)}) copy-start(bf16[768,768]{1,0:T(8,128)(2,1)} %param.17) | copy-start | bytes 3538948
  10.4 14.1 %all-to-all-start.1 = ((bf16[16,128,8]{1,2,0:T(8,128)(2,1)}), bf16[16,128,8]{1,2,0:T(8,128)(2,1)S(1)}, u32[]{:S(2)}, u32[]{:S(2)}) async-start(bf16[16,128,8]{1,2,0:T(8,128)(2,1)} %copy.69), calls=%async_computation.1 | async-start | bytes 65536 | tf_op jit(solution)/shard_map/all_to_all | solution.py:173
  17.8 3.4 %copy-start.5 = (f32[768]{0:T(1024)S(1)}, f32[768]{0:T(1024)}, u32[]{:S(2)}) copy-start(f32[768]{0:T(1024)} %param.16) | copy-start | bytes 9220
  21.1 0.9 copy-start.1
  23.3 7.2 %copy-start.8 = (s32[128]{0:T(128)S(1)}, s32[128]{0:T(128)}, u32[]{:S(2)}) copy-start(s32[128]{0:T(128)} %param.18) | copy-start | bytes 1540
  24.5 27.8 %all-to-all-start = ((bf16[16,5,48,128]{3,2,1,0:T(8,128)(2,1)}), bf16[16,5,48,128]{3,2,1,0:T(8,128)(2,1)S(1)}, u32[]{:S(2)}, u32[]{:S(2)}) async-start(bf16[16,5,48,128]{3,2,1,0:T(8,128)(2,1)} %copy.66), calls=%async_computation | async-start | bytes 1966080 | tf_op jit(solution)/shard_map/all_to_all | solution.py:179
  30.4 212.0 %reduce-scatter.4.cloned.1.call-start = ((), (), s32[]{:S(2)}) async-start(), calls=%async_computation.5 | async-start | bytes 12533760
  93.1 0.9 copy-start.2
  93.2 1.3 copy-start.3
  113.0 12.9 %copy-start.6 = (f32[128]{0:T(128)S(1)}, f32[128]{0:T(128)}, u32[]{:S(2)}) copy-start(f32[128]{0:T(128)} %param.13) | copy-start | bytes 1540
  113.0 12.9 %copy-start.7 = (f32[128,16]{0,1:T(8,128)S(1)}, f32[128,16]{0,1:T(8,128)}, u32[]{:S(2)}) copy-start(f32[128,16]{0,1:T(8,128)} %param.14) | copy-start | bytes 24580
  125.9 0.7 copy-start.4
Sparse Core Ops, SparseCore 0:
  113.2 129.1 reduce-scatter.3
where the time goes:
time: 254 us; the launch traced here: 253 us
  blocking collectives  102 us (40%)
  waiting for transfers between devices  69.8 us (27%)
  local copies, waits for them, and re-layouts  22.9 us (9%)
  matrix products  20.6 us (8%)
  between operations  14.4 us (6%)
  starting transfers between devices  13.4 us (5%)
  other arithmetic  9.52 us (4%)
    psum x1, blocking collectives, on_device(): lax.psum((query_part, weight_part, gain_part), 'tok')  60.7 us
    unnamed x2, waiting for transfers between devices  48 us
    all_to_all x1, blocking collectives, on_device(): lax.all_to_all(returned, 'tok', split_axis=0, concat_axis=0, tiled=True)  30 us
    all_to_all x1, waiting for transfers between devices, on_device(): lax.all_to_all(row_blocks(five_view, blocks), 'tok', split_axis=0, concat...  21.7 us
    unnamed x25, local copies, waits for them, and re-layouts  16.6 us
    all_to_all x1, blocking collectives, on_device(): lax.all_to_all(grad_bias_part[None].astype(jnp.bfloat16), 'tok', split_ax...  11.2 us
    all_to_all x1, starting transfers between devices, on_device(): lax.all_to_all(dest_order(bias_wide), 'tok', split_axis=0, concat_axis=2,...  7.41 us
    all_to_all x1, starting transfers between devices, on_device(): lax.all_to_all(row_blocks(five_view, blocks), 'tok', split_axis=0, concat...  5.91 us
  transfers between devices with their start and end apart: 3, of which 3 were waited for; matrix products, arithmetic and copies ran while one was open for 6% of the time, Pallas kernels for 0%

commit v1 on v0

v1 whole, which is shorter than its diff:
```python
import jax
import jax.numpy as jnp
from jax import lax
from jax.sharding import PartitionSpec as P

HEADS = 16
HD = 48
EPSILON = 1e-05
MASK_PENALTY = 10000.0
F32 = jnp.float32
BF16 = jnp.bfloat16


def attention(query, keys, values, gate, grad_gated, bias_t, key_bias):
    scale = HD ** (-0.5)
    scores = jnp.einsum("hdj,hdi->hji", keys, query, preferred_element_type=F32) * scale
    scores = scores + bias_t.transpose(1, 0, 2).astype(F32) + key_bias[None, :, None]
    peak = jnp.max(scores, axis=1, keepdims=True)
    expo = jnp.exp(scores - peak)
    probs = expo / jnp.sum(expo, axis=1, keepdims=True)
    probs_b = probs.astype(BF16)
    attended = jnp.einsum("hdj,hji->hdi", values, probs_b, preferred_element_type=F32).astype(BF16)
    gate32 = gate.astype(F32)
    grad32 = grad_gated.astype(F32)
    att32 = attended.astype(F32)
    gated = (gate32 * att32).astype(BF16)
    grad_att = (grad32 * gate32).astype(BF16)
    grad_logit = (grad32 * att32 * gate32 * (1.0 - gate32)).astype(BF16)
    grad_probs = jnp.einsum("hdj,hdi->hji", values, grad_att, preferred_element_type=F32)
    grad_scores = probs * (grad_probs - jnp.sum(probs * grad_probs, axis=1, keepdims=True))
    scores_b = grad_scores.astype(BF16)
    grad_query = (jnp.einsum("hdj,hji->hdi", keys, scores_b, preferred_element_type=F32) * scale).astype(BF16)
    grad_key = (jnp.einsum("hdi,hji->hdj", query, scores_b, preferred_element_type=F32) * scale).astype(BF16)
    grad_value = jnp.einsum("hdi,hji->hdj", grad_att, probs_b, preferred_element_type=F32).astype(BF16)
    return jnp.stack([grad_query, grad_key, grad_value, grad_logit]), gated, grad_scores


def on_device(activations, pair_repr, pair_gain, bias_weight, proj_weight, query_bias, out_weight, token_mask, out_cotangent):
    samples, tokens, feature = activations.shape
    tok = lax.axis_size("tok")
    cols = pair_repr.shape[1]
    act = activations.reshape(samples * tokens, feature)
    cot = out_cotangent.reshape(samples * tokens, feature)
    pair_f = pair_repr.astype(F32)
    centred = pair_f - jnp.mean(pair_f, axis=-1, keepdims=True)
    rstd = lax.rsqrt(jnp.mean(centred * centred, axis=-1, keepdims=True) + EPSILON)
    normed = centred * rstd
    scaled = normed * pair_gain
    bias_cols = jnp.einsum("ijc,ch->jhi", scaled, bias_weight, precision=lax.Precision.HIGHEST).astype(BF16)
    bias_t = lax.all_gather(bias_cols, "tok", axis=0, tiled=True)
    proj = jnp.einsum("tf,fn->nt", act, proj_weight, preferred_element_type=F32)
    proj = proj.reshape(4, feature, samples * tokens)
    query = (proj[0] + query_bias[:, None]).astype(BF16)
    keys = proj[1].astype(BF16)
    values = proj[2].astype(BF16)
    gate = jax.nn.sigmoid(proj[3]).astype(BF16)
    grad_gated = jnp.einsum("tn,mn->mt", cot, out_weight, preferred_element_type=F32).astype(BF16)
    key_bias = (token_mask.astype(F32) - 1.0) * MASK_PENALTY

    def heads_of(x):
        return x.reshape(HEADS, HD, samples, tokens).transpose(2, 0, 1, 3)

    grads, gated, grad_scores = jax.vmap(attention, in_axes=(0, 0, 0, 0, 0, None, None))(
        heads_of(query), heads_of(keys), heads_of(values), heads_of(gate), heads_of(grad_gated), bias_t, key_bias
    )
    grad_rows = grads.transpose(1, 2, 3, 0, 4).reshape(4 * feature, samples * tokens)
    gated_t = gated.transpose(1, 2, 0, 3).reshape(feature, samples * tokens)
    first = jnp.einsum("tr,nt->rn", act, grad_rows, preferred_element_type=F32)
    second = jnp.einsum("rt,tn->rn", gated_t, cot, preferred_element_type=F32)
    terms = jnp.concatenate([first.astype(BF16), second.astype(BF16)], axis=1)
    score_sum = jnp.sum(grad_scores, axis=0).astype(BF16)
    outgoing = score_sum.reshape(HEADS, tok, cols, tokens).transpose(1, 2, 0, 3)
    received = lax.all_to_all(outgoing, "tok", split_axis=0, concat_axis=0, tiled=True)
    grad_bias = jnp.sum(received.astype(F32), axis=0)
    grad_activations = jnp.einsum("nt,fn->tf", grad_rows, proj_weight, preferred_element_type=F32).astype(BF16)
    grad_zg = jnp.einsum("jhi,ch->ijc", grad_bias, bias_weight, precision=lax.Precision.HIGHEST)
    weight_part = jnp.einsum("ijc,jhi->ch", scaled, grad_bias, precision=lax.Precision.HIGHEST)
    gain_part = jnp.sum(normed * grad_zg, axis=(0, 1))
    query_part = jnp.sum(grad_rows[:feature].astype(F32), axis=1)
    small = jnp.concatenate([query_part, weight_part.reshape(-1), gain_part])
    small = jnp.sum(lax.all_gather(small, "tok", axis=0), axis=0)
    terms, small = lax.optimization_barrier((terms, small))
    weight_grads = lax.psum_scatter(terms, "tok", scatter_dimension=0, tiled=True).astype(F32)
    grad_norm = grad_zg * pair_gain
    grad_pair = (
        grad_norm
        - jnp.mean(grad_norm, axis=-1, keepdims=True)
        - normed * jnp.mean(grad_norm * normed, axis=-1, keepdims=True)
    ) * rstd
    split = feature + weight_part.size
    return (
        grad_activations.reshape(samples, tokens, feature),
        grad_pair.astype(BF16),
        weight_grads[:, : 4 * feature],
        weight_grads[:, 4 * feature :],
        small[:feature],
        small[feature:split].reshape(weight_part.shape),
        small[split:],
    )


def solution(mesh):
    in_specs = (
        P(("groups", "tok"), None, None),
        P("groups", "tok", None),
        P(),
        P(),
        P(),
        P(),
        P(),
        P("groups"),
        P(("groups", "tok"), None, None),
    )
    out_specs = (
        P(("groups", "tok"), None, None),
        P("groups", "tok", None),
        P(("groups", "tok"), None),
        P(("groups", "tok"), None),
        P("groups"),
        P("groups", None),
        P("groups"),
    )
    return jax.shard_map(on_device, mesh=mesh, in_specs=in_specs, out_specs=out_specs, check_vma=False)
```

time: 254 us -> 188 us (0.74)
  blocking collectives: 102 us -> 46.9 us
  starting transfers between devices: 13.4 us -> 4.28 us
  local copies, waits for them, and re-layouts: 22.9 us -> 19.2 us
    psum x1 -> x0, blocking collectives: 60.7 us -> none  [on_device(): lax.psum((query_part, weight_part, gain_part), 'tok')]
    all_gather x0 -> x2, blocking collectives: none -> 46.9 us  [the longest x1 24.6 us: on_device(): bias_t = lax.all_gather(bias_cols, 'tok', axis=0, tiled=True)]
    all_to_all x2 -> x0, blocking collectives: 41.2 us -> none  [the longest x1 30 us: on_device(): lax.all_to_all(returned, 'tok', split_axis=0, concat_axis=0, tiled=True)]
    unnamed x2, waiting for transfers between devices: 48 us -> 72.1 us
    all_to_all x2 -> x1, waiting for transfers between devices: 21.8 us -> 0.01 us  [on_device(): lax.all_to_all(outgoing, 'tok', split_axis=0, concat_axis=0, tiled=True)]
    all_to_all x2 -> x1, starting transfers between devices: 13.3 us -> 4.24 us  [on_device(): lax.all_to_all(outgoing, 'tok', split_axis=0, concat_axis=0, tiled=True)]
    dot_general x28 -> x14, matrix products: 19.4 us -> 22.6 us  [the longest x1 4.71 us: on_device(): jnp.einsum('nt,fn->tf', grad_rows, proj_weight, preferred_element_type=F32)]
    dynamic_update_slice x4 -> x0, other arithmetic: 2.84 us -> none  [on_device(): lax.scan(sample_step, start_total, grouped(head_items, group_size))]
  transfers between devices with their start and end apart: 3 -> 2, of which waited for: 3 -> 1; matrix products, arithmetic and copies ran while one was open for 6% -> 12% of each run, Pallas kernels for 0% -> 0%
where the time goes in v1:
time: 188 us; the launch traced here: 187 us
  waiting for transfers between devices  72.1 us (38%)
  blocking collectives  46.9 us (25%)
  matrix products  22.6 us (12%)
  local copies, waits for them, and re-layouts  19.2 us (10%)
  between operations  14.3 us (8%)
  other arithmetic  7.68 us (4%)
  starting transfers between devices  4.28 us (2%)
    unnamed x2, waiting for transfers between devices  72.1 us
    all_gather x1, blocking collectives, on_device(): bias_t = lax.all_gather(bias_cols, 'tok', axis=0, tiled=True)  24.6 us
    all_gather x1, blocking collectives, on_device(): small = jnp.sum(lax.all_gather(small, 'tok', axis=0), axis=0)  22.3 us
    unnamed x25, local copies, waits for them, and re-layouts  14.3 us
    dot_general x1, matrix products, on_device(): jnp.einsum('nt,fn->tf', grad_rows, proj_weight, preferred_element_type=F32)  4.71 us
    all_to_all x1, starting transfers between devices, on_device(): lax.all_to_all(outgoing, 'tok', split_axis=0, concat_axis=0, tiled=True)  4.24 us
    dot_general x1, matrix products, on_device(): proj = jnp.einsum('tf,fn->nt', act, proj_weight, preferred_element_type=F32)  3.8 us
  transfers between devices with their start and end apart: 2, of which 1 were waited for; matrix products, arithmetic and copies ran while one was open for 12% of the time, Pallas kernels for 0%

profile of v1, /device:TPU:0, one launch (start us, length us, event | category | flops | bytes accessed | tf_op | source)
XLA Modules:
  0.0 187.2 jit_solution(9706991575136482138)
XLA Ops:
  8.7 1.2 copy.32
  10.0 1.2 fusion.19
  11.2 24.6 %all_gather.9 = bf16[128,16,128]{2,0,1:T(8,128)(2,1)S(1)} all-gather(bf16[8,16,128]{2,0,1:T(8,128)(2,1)S(1)} %bitcast.85), channel_id=1, replica_groups=mesh['groups'=2,'tok'=16] {'tok'}, dimensions={0}, use_global_device_ids=true | all-gather | bytes 557056 | tf_op jit(solution)/shard_map/all_gather | solution.py:50
  35.9 3.8 %fusion.59 = (bf16[3072,128]{1,0:T(8,128)(2,1)S(1)}, f32[3072,128]{1,0:T(8,128)S(1)}) fusion(bf16[768,3072]{1,0:T(8,128)(2,1)} %param.13, bf16[1,128,768]{2,1,0:T(8,128)(2,1)} %param.9), kind=kOutput, calls=%fused_computation.91 | convolution fusion | flops 604372992 | bytes 7274496 | tf_op jit(solution)/shard_map/tf,fn->nt/dot_general | solution.py:51
  40.4 1.0 fusion.60
  42.8 0.9 copy_bitcast_fusion
  43.7 4.2 %all-to-all-start = ((bf16[16,8,16,128]{3,1,2,0:T(8,128)(2,1)}), bf16[16,8,16,128]{3,1,2,0:T(8,128)(2,1)}, u32[]{:S(2)}, u32[]{:S(2)}) async-start(bf16[16,8,16,128]{3,1,2,0:T(8,128)(2,1)} %copy_bitcast_fusion), calls=%async_computation | async-start | bytes 1048576 | tf_op jit(solution)/shard_map/all_to_all | solution.py:73
  48.0 2.2 %fusion.10 = bf16[1,1,16,48,128]{4,3,2,1,0:T(8,128)(2,1)} fusion(bf16[16,48,128]{2,1,0:T(8,128)(2,1)} %bitcast.83, bf16[16,48,128]{2,1,0:T(8,128)(2,1)} %bitcast.77, f32[16,128]{1,0:T(8,128)S(1)} %get-tuple-element.43, f32[16,128,128]{2,1,0:T(8,128)S(1)} %fusion.5), kind=kOutput, calls=%fused_computation.21 | convolution fusion | flops 26445952 | bytes 1646592 | tf_op jit(solution)/shard_map/vmap(hdi,hji->hdj)/dot_general | solution.py:34
  50.2 2.3 %fusion.30 = (bf16[16,48,128]{2,1,0:T(8,128)(2,1)}, bf16[1,1,16,48,128]{4,3,2,1,0:T(8,128)(2,1)}) fusion(bf16[16,48,128]{2,1,0:T(8,128)(2,1)} %bitcast.84, bf16[16,48,128]{2,1,0:T(8,128)(2,1)} %bitcast.78, bf16[16,48,128]{2,1,0:T(8,128)(2,1)} %bitcast.81, f32[16,128]{1,0:T(8,128)S(1)} %get-tuple-element.43, f32[16,128,128]{2,1,0:T(8,128)S(1)} %fusion.5), kind=kOutput, calls=%fused_computation.54 | convolution fusion | flops 27035776 | bytes 2039808 | tf_op jit(solution)/shard_map/vmap(hdj,hji->hdi)/dot_general | solution.py:22
  53.0 1.3 convert_reduce_fusion.2
  54.3 1.5 convolution_convert_fusion.1
  55.8 1.1 pad_maximum_fusion.1
  57.0 2.3 %fusion.1 = bf16[768,3072]{0,1:T(8,128)(2,1)S(1)} fusion(bf16[3072,128]{1,0:T(8,128)(2,1)S(1)} %bitcast.69, bf16[1,128,768]{2,1,0:T(8,128)(2,1)} %param.9), kind=kOutput, calls=%fused_computation.3 | convolution fusion | flops 606339072 | bytes 5701632 | tf_op jit(solution)/shard_map/tr,nt->rn/dot_general | solution.py:68
  59.3 2.9 %pad_maximum_fusion = bf16[768,3840]{0,1:T(8,128)(2,1)} fusion(bf16[768,768]{0,1:T(8,128)(2,1)S(1)} %convolution_convert_fusion.1, bf16[768,3072]{0,1:T(8,128)(2,1)S(1)} %fusion.1), kind=kLoop, calls=%fused_computation.1 | loop fusion | flops 11796480 | bytes 11796480 | tf_op jit(solution)/shard_map/concatenate | solution.py:70
  62.2 1.1 convert_reduce_fusion
  64.0 0.8 fusion.25
  64.9 22.3 %all-gather.1 = f32[16,1,2944]{2,1,0:T(1,128)S(1)} all-gather(f32[1,1,2944]{2,1,0:T(1,128)S(1)} %reshape.198), channel_id=2, replica_groups=mesh['groups'=2,'tok'=16] {'tok'}, dimensions={0}, use_global_device_ids=true | all-gather | bytes 200192 | tf_op jit(solution)/shard_map/all_gather | solution.py:81
  87.4 8.5 %copy.49 = bf16[768,3840]{1,0:T(8,128)(2,1)} copy(bf16[768,3840]{0,1:T(8,128)(2,1)} %pad_maximum_fusion) | data formatting | bytes 11796480
  95.9 4.7 %fusion.11 = bf16[1,128,768]{2,1,0:T(8,128)(2,1)} fusion(bf16[3072,128]{1,0:T(8,128)(2,1)S(1)} %bitcast.70, bf16[768,3072]{1,0:T(8,128)(2,1)} %param.13), kind=kOutput, calls=%fused_computation.22 | convolution fusion | flops 604078080 | bytes 5701632 | tf_op jit(solution)/shard_map/nt,fn->tf/dot_general | solution.py:75
  102.0 0.9 copy.41
  103.6 72.1 %reduce-scatter.4.cloned.1.call-done = bf16[48,3840]{1,0:T(8,128)(2,1)} async-done(((bf16[768,3840]{1,0:T(8,128)(2,1)}), bf16[48,3840]{1,0:T(8,128)(2,1)}) %reduce-scatter.4.cloned.1.call-update) | async-done | bytes 368656
  175.7 0.9 slice.57
  177.6 1.0 slice.56
  179.1 1.3 copy.42
  (49 shorter events, 8.6 us)
Async XLA Ops:
  7.2 34.2 %copy-start = (bf16[768,768]{1,0:T(8,128)(2,1)S(1)}, bf16[768,768]{1,0:T(8,128)(2,1)}, u32[]{:S(2)}) copy-start(bf16[768,768]{1,0:T(8,128)(2,1)} %param.15) | copy-start | bytes 3538948
  39.7 1.8 copy-start.2
  39.7 2.6 %copy-start.4 = (bf16[768,128]{1,0:T(8,128)(2,1)}, bf16[768,128]{1,0:T(8,128)(2,1)S(1)}, u32[]{:S(2)}) copy-start(bf16[768,128]{1,0:T(8,128)(2,1)S(1)} %get-tuple-element.38) | copy-start | bytes 589828
  39.7 2.6 %copy-start.1 = (bf16[768,128]{1,0:T(8,128)(2,1)}, bf16[768,128]{1,0:T(8,128)(2,1)S(1)}, u32[]{:S(2)}) copy-start(bf16[768,128]{1,0:T(8,128)(2,1)S(1)} %get-tuple-element.37) | copy-start | bytes 589828
  39.8 2.5 %copy-start.5 = (bf16[768,128]{1,0:T(8,128)(2,1)}, bf16[768,128]{1,0:T(8,128)(2,1)S(1)}, u32[]{:S(2)}) copy-start(bf16[768,128]{1,0:T(8,128)(2,1)S(1)} %get-tuple-element.36) | copy-start | bytes 589828
  41.9 0.7 copy-start.3
  43.7 18.5 %all-to-all-start = ((bf16[16,8,16,128]{3,1,2,0:T(8,128)(2,1)}), bf16[16,8,16,128]{3,1,2,0:T(8,128)(2,1)}, u32[]{:S(2)}, u32[]{:S(2)}) async-start(bf16[16,8,16,128]{3,1,2,0:T(8,128)(2,1)} %copy_bitcast_fusion), calls=%async_computation | async-start | bytes 1048576 | tf_op jit(solution)/shard_map/all_to_all | solution.py:73
  48.0 127.8 %reduce-scatter.4.cloned.1.call-start = ((), (), s32[]{:S(2)}) async-start(), calls=%async_computation.2 | async-start | bytes 6266880
  59.3 4.1 %copy-start.6 = (f32[128]{0:T(128)S(1)}, f32[128]{0:T(128)}, u32[]{:S(2)}) copy-start(f32[128]{0:T(128)} %param.11) | copy-start | bytes 1540
  59.3 4.7 %copy-start.7 = (f32[128,16]{0,1:T(8,128)S(1)}, f32[128,16]{0,1:T(8,128)}, u32[]{:S(2)}) copy-start(f32[128,16]{0,1:T(8,128)} %param.12) | copy-start | bytes 24580
Sparse Core Ops, SparseCore 0:
  96.1 79.6 reduce-scatter.3

commit v2 on v1

--- a/solution.py
+++ b/solution.py
@@ -1,6 +1,10 @@
+import functools
+
 import jax
 import jax.numpy as jnp
 from jax import lax
+from jax.experimental import pallas as pl
+from jax.experimental.pallas import tpu as pltpu
 from jax.sharding import PartitionSpec as P
 
 HEADS = 16
@@ -9,6 +13,84 @@
 MASK_PENALTY = 10000.0
 F32 = jnp.float32
 BF16 = jnp.bfloat16
+INNER = 4
+
+
+def exchange_kernel(kinds, tok, *refs):
+    count = len(kinds)
+    ins, outs = refs[:count], refs[count : 2 * count]
+    sends, recvs, local_sem = refs[2 * count : 3 * count], refs[3 * count : 4 * count], refs[4 * count]
+    me = lax.axis_index("tok")
+    group = me // INNER
+    place = me % INNER
+    across = place + 1 - 2 * (place % 2)
+    beside = place + 2 - 4 * (place // 2)
+    barrier = pltpu.get_barrier_semaphore()
+    for step in range(1, tok):
+        pl.semaphore_signal(barrier, inc=1, device_id={"tok": (me + step) % tok})
+    pl.semaphore_wait(barrier, tok - 1)
+
+    def send(k, slot, src, dst, peer):
+        copy = pltpu.make_async_remote_copy(
+            src_ref=src,
+            dst_ref=dst,
+            send_sem=sends[k].at[slot],
+            recv_sem=recvs[k].at[slot],
+            device_id={"tok": peer},
+        )
+        copy.start()
+        return copy
+
+    pending, relays, local = [], [], []
+    for k, kind in enumerate(kinds):
+        x, out = ins[k], outs[k]
+        if kind == "near":
+            first = send(k, 0, x, out.at[place], group * INNER + beside)
+            pending.append(send(k, 1, x, out.at[place], group * INNER + across))
+            relays.append((k, first, out.at[beside]))
+        elif kind in ("all", "each"):
+            for step in range(1, tok):
+                peer = (me + step) % tok
+                pending.append(send(k, step - 1, x if kind == "all" else x.at[peer], out.at[me], peer))
+        elif kind == "near_each":
+            for step in range(1, INNER):
+                other = (place + step) % INNER
+                pending.append(send(k, step - 1, x.at[other], out.at[place], group * INNER + other))
+        else:
+            for step in range(1, tok // INNER):
+                other = (group + step) % (tok // INNER)
+                pending.append(send(k, step - 1, x.at[other], out.at[group], other * INNER + place))
+    for k, kind in enumerate(kinds):
+        mine = {"all": me, "each": me, "near": place, "near_each": place, "far_each": group}[kind]
+        own = ins[k] if kind in ("all", "near") else ins[k].at[mine]
+        copy = pltpu.make_async_copy(own, outs[k].at[mine], local_sem.at[k])
+        copy.start()
+        local.append(copy)
+    for k, first, block in relays:
+        first.wait()
+        pending.append(send(k, 2, block, block, group * INNER + across))
+    for copy in local + pending:
+        copy.wait()
+
+
+def exchange(arrays, kinds, tok, collective_id):
+    sizes = {"all": tok, "each": tok, "near": INNER, "near_each": INNER, "far_each": tok // INNER}
+    shapes = []
+    for x, kind in zip(arrays, kinds):
+        block = x.shape if kind in ("all", "near") else x.shape[1:]
+        shapes.append(jax.ShapeDtypeStruct((sizes[kind],) + block, x.dtype))
+    sems = [pltpu.SemaphoreType.DMA((max(3, sizes[kind] - 1),)) for kind in kinds]
+    return pl.pallas_call(
+        functools.partial(exchange_kernel, kinds, tok),
+        out_shape=shapes,
+        in_specs=[pl.BlockSpec(memory_space=pltpu.VMEM)] * len(kinds),
+        out_specs=[pl.BlockSpec(memory_space=pltpu.VMEM)] * len(kinds),
+        scratch_shapes=sems + sems + [pltpu.SemaphoreType.DMA((len(kinds),))],
+        compiler_params=pltpu.CompilerParams(
+            collective_id=collective_id, has_side_effects=True, vmem_limit_bytes=40 * 2**20
+        ),
+        name=f"exchange_{collective_id}",
+    )(*arrays)
 
 
 def attention(query, keys, values, gate, grad_gated, bias_t, key_bias):
@@ -47,7 +129,17 @@
     normed = centred * rstd
     scaled = normed * pair_gain
     bias_cols = jnp.einsum("ijc,ch->jhi", scaled, bias_weight, precision=lax.Precision.HIGHEST).astype(BF16)
-    bias_t = lax.all_gather(bias_cols, "tok", axis=0, tiled=True)
+    outer = tok // INNER
+    shard = feature // tok
+
+    def near_blocks(x):
+        blocks = x.reshape(outer, INNER, shard, samples * tokens).transpose(1, 0, 2, 3)
+        return blocks.reshape(INNER, outer * shard, samples * tokens)
+
+    bias_t, cot_near, act_near = exchange(
+        (bias_cols, cot, near_blocks(act.T)), ("all", "near", "near_each"), tok, 0
+    )
+    bias_t = bias_t.reshape((tok * cols,) + bias_cols.shape[1:])
     proj = jnp.einsum("tf,fn->nt", act, proj_weight, preferred_element_type=F32)
     proj = proj.reshape(4, feature, samples * tokens)
     query = (proj[0] + query_bias[:, None]).astype(BF16)
@@ -65,12 +157,11 @@
     )
     grad_rows = grads.transpose(1, 2, 3, 0, 4).reshape(4 * feature, samples * tokens)
     gated_t = gated.transpose(1, 2, 0, 3).reshape(feature, samples * tokens)
-    first = jnp.einsum("tr,nt->rn", act, grad_rows, preferred_element_type=F32)
-    second = jnp.einsum("rt,tn->rn", gated_t, cot, preferred_element_type=F32)
-    terms = jnp.concatenate([first.astype(BF16), second.astype(BF16)], axis=1)
     score_sum = jnp.sum(grad_scores, axis=0).astype(BF16)
     outgoing = score_sum.reshape(HEADS, tok, cols, tokens).transpose(1, 2, 0, 3)
-    received = lax.all_to_all(outgoing, "tok", split_axis=0, concat_axis=0, tiled=True)
+    received, rows_near, gated_near = exchange(
+        (outgoing, grad_rows, near_blocks(gated_t)), ("each", "near", "near_each"), tok, 1
+    )
     grad_bias = jnp.sum(received.astype(F32), axis=0)
     grad_activations = jnp.einsum("nt,fn->tf", grad_rows, proj_weight, preferred_element_type=F32).astype(BF16)
     grad_zg = jnp.einsum("jhi,ch->ijc", grad_bias, bias_weight, precision=lax.Precision.HIGHEST)
@@ -78,9 +169,13 @@
     gain_part = jnp.sum(normed * grad_zg, axis=(0, 1))
     query_part = jnp.sum(grad_rows[:feature].astype(F32), axis=1)
     small = jnp.concatenate([query_part, weight_part.reshape(-1), gain_part])
-    small = jnp.sum(lax.all_gather(small, "tok", axis=0), axis=0)
-    terms, small = lax.optimization_barrier((terms, small))
-    weight_grads = lax.psum_scatter(terms, "tok", scatter_dimension=0, tiled=True).astype(F32)
+    small = jnp.pad(small, (0, -small.size % 1024)).reshape(-1, 128)
+    first = jnp.einsum("srt,snt->rn", act_near, rows_near, preferred_element_type=F32)
+    second = jnp.einsum("srt,stn->rn", gated_near, cot_near, preferred_element_type=F32)
+    terms = jnp.concatenate([first.astype(BF16), second.astype(BF16)], axis=1)
+    terms, small = exchange((terms.reshape(outer, shard, -1), small), ("far_each", "all"), tok, 2)
+    weight_grads = jnp.sum(terms.astype(F32), axis=0)
+    small = jnp.sum(small, axis=0).reshape(-1)
     grad_norm = grad_zg * pair_gain
     grad_pair = (
         grad_norm
@@ -95,7 +190,7 @@
         weight_grads[:, 4 * feature :],
         small[:feature],
         small[feature:split].reshape(weight_part.shape),
-        small[split:],
+        small[split : split + pair_gain.shape[0]],
     )
 
 

time: 188 us -> 133 us (0.71)
  Pallas kernels: 0 us -> 89 us
  waiting for transfers between devices: 72.1 us -> 0 us
  blocking collectives: 46.9 us -> 0 us
  between operations: 14.3 us -> 1.01 us
  local copies, waits for them, and re-layouts: 19.2 us -> 12.6 us
  starting transfers between devices: 4.28 us -> 0 us
  other arithmetic: 7.68 us -> 4.7 us
  matrix products: 22.6 us -> 24.8 us
    pallas_call x0 -> x3, Pallas kernels: none -> 89 us  [exchange(): pl.pallas_call(functools.partial(exchange_kernel, kinds, tok), out_shape=...]
    unnamed x2 -> x0, waiting for transfers between devices: 72.1 us -> none
    all_gather x2 -> x0, blocking collectives: 46.9 us -> none  [the longest x1 24.6 us: on_device(): bias_t = lax.all_gather(bias_cols, 'tok', axis=0, tiled=True)]
    unnamed x25 -> x34, local copies, waits for them, and re-layouts: 14.3 us -> 6.94 us
    all_to_all x1 -> x0, starting transfers between devices: 4.24 us -> none  [on_device(): lax.all_to_all(outgoing, 'tok', split_axis=0, concat_axis=0, tiled=True)]
    concatenate x1, other arithmetic: 2.9 us -> 0.1 us  [on_device(): terms = jnp.concatenate([first.astype(BF16), second.astype(BF16)], axis=1)]
  transfers between devices with their start and end apart: 2 -> 0, of which waited for: 1 -> 0; matrix products, arithmetic and copies ran while one was open for 12% -> 0% of each run, Pallas kernels for 0% -> 0%
where the time goes in v2:
time: 133 us; the launch traced here: 132 us
  Pallas kernels  89 us (67%)
  matrix products  24.8 us (19%)
  local copies, waits for them, and re-layouts  12.6 us (9%)
  other arithmetic  4.7 us (4%)
    pallas_call x3, Pallas kernels, exchange(): pl.pallas_call(functools.partial(exchange_kernel, kinds, tok), out_shape=...  89 us
    unnamed x34, local copies, waits for them, and re-layouts  6.94 us
    dot_general x1, matrix products, on_device(): jnp.einsum('nt,fn->tf', grad_rows, proj_weight, preferred_element_type=F32)  4.72 us
    dot_general x1, matrix products, on_device(): proj = jnp.einsum('tf,fn->nt', act, proj_weight, preferred_element_type=F32)  3.79 us
    dot_general x1, matrix products, on_device(): jnp.einsum('srt,snt->rn', act_near, rows_near, preferred_element_type=F32)  3.06 us
    dot_general x1, matrix products, attention(): jnp.einsum('hdi,hji->hdj', grad_att, probs_b, preferred_element_type=F32)  2.96 us
    dot_general x1, matrix products, attention(): jnp.einsum('hdj,hji->hdi', values, probs_b, preferred_element_type=F32)  2.88 us

profile of v2, /device:TPU:0, one launch (start us, length us, event | category | flops | bytes accessed | tf_op | source)
XLA Modules:
  0.0 132.1 jit_solution(13464545769975276038)
XLA Ops:
  0.7 0.8 add_multiply_fusion
  1.5 0.8 add.48
  2.2 2.1 %convolution_convert_fusion.3 = bf16[768,128]{1,0:T(8,128)(2,1)} fusion(bf16[768,768]{1,0:T(8,128)(2,1)S(1)} %copy-done, bf16[1,128,768]{2,1,0:T(8,128)(2,1)} %param.17), kind=kOutput, calls=%fused_computation.19 | convolution fusion | flops 151093248 | bytes 1572864 | tf_op jit(solution)/shard_map/tn,mn->mt/dot_general | solution.py:149
  4.3 1.2 copy.24
  7.0 19.0 %exchange_0.1 = (bf16[16,8,16,128]{3,2,1,0:T(8,128)(2,1)S(1)}, bf16[4,128,768]{2,1,0:T(8,128)(2,1)S(1)}, bf16[4,192,128]{2,1,0:T(8,128)(2,1)S(1)}) custom-call(bf16[8,16,128]{2,1,0:T(8,128)(2,1)S(1)} %fusion.13.refs_0_, bf16[128,768]{1,0:T(8,128)(2,1)S(1)} %bitcast.96, bf16[4,192,128]{2,1,0:T(8,128)(2,1)S(1)} %bitcast.97), custom_call_target="tpu_custom_call" | custom-call | tf_op jit(solution)/shard_map/exchange_0/pallas_call | solution.py:83
  26.0 3.8 %fusion.56 = (bf16[3072,128]{1,0:T(8,128)(2,1)S(1)}, f32[3072,128]{1,0:T(8,128)S(1)}) fusion(bf16[768,3072]{1,0:T(8,128)(2,1)} %param.13, bf16[1,128,768]{2,1,0:T(8,128)(2,1)S(1)} %copy-done.10), kind=kOutput, calls=%fused_computation.93 | convolution fusion | flops 604372992 | bytes 7274496 | tf_op jit(solution)/shard_map/tf,fn->nt/dot_general | solution.py:143
  30.5 0.8 fusion.54
  31.3 0.7 fusion.5
  32.1 1.0 copy-done.3
  33.1 0.9 fusion.57
  34.0 3.0 %fusion.11 = bf16[1,1,16,48,128]{4,3,2,1,0:T(8,128)(2,1)} fusion(bf16[16,48,128]{2,1,0:T(8,128)(2,1)} %bitcast.111, bf16[16,48,128]{2,1,0:T(8,128)(2,1)} %bitcast.105, f32[16,128]{1,0:T(8,128)S(1)} %get-tuple-element.48, f32[16,128,128]{2,1,0:T(8,128)} %copy-done.3), kind=kOutput, calls=%fused_computation.23 | convolution fusion | flops 26445952 | bytes 1646592 | tf_op jit(solution)/shard_map/vmap(hdi,hji->hdj)/dot_general | solution.py:116
  37.0 2.9 %fusion.31 = (bf16[16,48,128]{2,1,0:T(8,128)(2,1)}, bf16[1,1,16,48,128]{4,3,2,1,0:T(8,128)(2,1)}) fusion(bf16[16,48,128]{2,1,0:T(8,128)(2,1)} %bitcast.112, bf16[16,48,128]{2,1,0:T(8,128)(2,1)S(1)} %bitcast.107, bf16[16,48,128]{2,1,0:T(8,128)(2,1)} %bitcast.109, f32[16,128]{1,0:T(8,128)S(1)} %get-tuple-element.48, f32[16,128,128]{2,1,0:T(8,128)} %copy-done.3), kind=kOutput, calls=%fused_computation.57 | convolution fusion | flops 27035776 | bytes 2039808 | tf_op jit(solution)/shard_map/vmap(hdj,hji->hdi)/dot_general | solution.py:104
  39.9 0.9 copy.30
  40.8 1.5 %multiply_reduce_fusion = (f32[16,128]{1,0:T(8,128)S(1)}, f32[16,128,128]{2,1,0:T(8,128)S(1)}) fusion(f32[16,128,128]{2,1,0:T(8,128)S(1)} %get-tuple-element.49, f32[16,128]{1,0:T(8,128)S(1)} %get-tuple-element.48, bf16[16,48,128]{2,1,0:T(8,128)(2,1)} %bitcast.110, bf16[16,48,128]{2,1,0:T(8,128)(2,1)} %bitcast.113, bf16[16,48,128]{2,1,0:T(8,128)(2,1)} %bitcast.106), kind=kOutput, calls=%fused_computation.30 | convolution fusion | flops 26343424 | bytes 2703360 | tf_op jit(solution)/shard_map/vmap(hdj,hdi->hji)/dot_general | solution.py:111
  42.6 0.8 copy-done.7
  44.6 1.1 pad_maximum_fusion.1
  45.7 4.7 %fusion.12 = bf16[1,128,768]{2,1,0:T(8,128)(2,1)} fusion(bf16[3072,128]{1,0:T(8,128)(2,1)S(1)} %bitcast.92, bf16[768,3072]{1,0:T(8,128)(2,1)} %param.13), kind=kOutput, calls=%fused_computation.24 | convolution fusion | flops 604078080 | bytes 5701632 | tf_op jit(solution)/shard_map/nt,fn->tf/dot_general | solution.py:166
  50.5 29.7 %exchange_1.1 = (bf16[16,8,16,128]{3,2,1,0:T(8,128)(2,1)S(1)}, bf16[4,3072,128]{2,1,0:T(8,128)(2,1)S(1)}, bf16[4,192,128]{2,1,0:T(8,128)(2,1)S(1)}) custom-call(bf16[16,8,16,128]{3,2,1,0:T(8,128)(2,1)S(1)} %bitcast.95, bf16[3072,128]{1,0:T(8,128)(2,1)S(1)} %bitcast.93, bf16[4,192,128]{2,1,0:T(8,128)(2,1)S(1)} %bitcast.98), custom_call_target="tpu_custom_call" | custom-call | tf_op jit(solution)/shard_map/exchange_1/pallas_call | solution.py:83
  80.2 1.7 %copy-done.1 = bf16[4,3072,128]{2,1,0:T(8,128)(2,1)} copy-done((bf16[4,3072,128]{2,1,0:T(8,128)(2,1)}, bf16[4,3072,128]{2,1,0:T(8,128)(2,1)S(1)}, u32[]{:S(2)}) %copy-start.1) | copy-done | bytes 3145752
  82.9 0.8 fusion.26
  84.0 0.9 copy.33
  84.9 3.1 %fusion.1 = bf16[192,3072]{1,0:T(8,128)(2,1)S(1)} fusion(bf16[4,192,128]{2,1,0:T(8,128)(2,1)S(1)} %get-tuple-element.17, bf16[4,3072,128]{2,1,0:T(8,128)(2,1)} %copy-done.1), kind=kOutput, calls=%fused_computation.2 | convolution fusion | flops 604569600 | bytes 4521984 | tf_op jit(solution)/shard_map/srt,snt->rn/dot_general | solution.py:173
  88.0 40.4 %exchange_2.1 = (bf16[4,48,3840]{2,1,0:T(8,128)(2,1)S(1)}, f32[16,24,128]{2,1,0:T(8,128)S(1)}) custom-call(bf16[4,48,3840]{2,1,0:T(8,128)(2,1)S(1)} %bitcast.94, f32[24,128]{1,0:T(8,128)S(1)} %fusion.50.refs_1_), custom_call_target="tpu_custom_call" | custom-call | tf_op jit(solution)/shard_map/exchange_2/pallas_call | solution.py:83
  131.3 0.9 slice.57
  (57 shorter events, 7.9 us)
Async XLA Ops:
  0.6 1.6 %copy-start = (bf16[768,768]{1,0:T(8,128)(2,1)S(1)}, bf16[768,768]{1,0:T(8,128)(2,1)}, u32[]{:S(2)}) copy-start(bf16[768,768]{1,0:T(8,128)(2,1)} %param.15) | copy-start | bytes 3538948
  0.6 5.8 %copy-start.13 = (f32[128]{0:T(128)S(1)}, f32[128]{0:T(128)}, u32[]{:S(2)}) copy-start(f32[128]{0:T(128)} %param.11) | copy-start | bytes 1540
  0.7 6.3 %copy-start.2 = (bf16[1,128,768]{2,1,0:T(8,128)(2,1)S(1)}, bf16[1,128,768]{2,1,0:T(8,128)(2,1)}, u32[]{:S(2)}) copy-start(bf16[1,128,768]{2,1,0:T(8,128)(2,1)} %param.17) | copy-start | bytes 589828
  0.7 5.8 %copy-start.14 = (f32[128,16]{0,1:T(8,128)S(1)}, f32[128,16]{0,1:T(8,128)}, u32[]{:S(2)}) copy-start(f32[128,16]{0,1:T(8,128)} %param.12) | copy-start | bytes 24580
  0.7 4.8 %copy-start.11 = (bf16[128,8,128]{2,1,0:T(8,128)(2,1)S(1)}, bf16[128,8,128]{2,1,0:T(8,128)(2,1)}, u32[]{:S(2)}) copy-start(bf16[128,8,128]{2,1,0:T(8,128)(2,1)} %param.10) | copy-start | bytes 786436
  4.3 21.7 %copy-start.10 = (bf16[1,128,768]{2,1,0:T(8,128)(2,1)S(1)}, bf16[1,128,768]{2,1,0:T(8,128)(2,1)}, u32[]{:S(2)}) copy-start(bf16[1,128,768]{2,1,0:T(8,128)(2,1)} %param.9) | copy-start | bytes 589828
  5.7 0.7 copy-start.4
  30.5 3.5 %copy-start.8 = (bf16[768,128]{1,0:T(8,128)(2,1)}, bf16[768,128]{1,0:T(8,128)(2,1)S(1)}, u32[]{:S(2)}) copy-start(bf16[768,128]{1,0:T(8,128)(2,1)S(1)} %get-tuple-element.42) | copy-start | bytes 589828
  31.3 2.7 %copy-start.6 = (f32[768,128]{1,0:T(8,128)}, f32[768,128]{1,0:T(8,128)S(1)}, u32[]{:S(2)}) copy-start(f32[768,128]{1,0:T(8,128)S(1)} %get-tuple-element.40) | copy-start | bytes 1179652
  32.1 1.0 copy-start.3
  34.0 3.0 %copy-start.12 = (bf16[768,128]{1,0:T(8,128)(2,1)S(1)}, bf16[768,128]{1,0:T(8,128)(2,1)}, u32[]{:S(2)}) copy-start(bf16[768,128]{1,0:T(8,128)(2,1)} %convolution_convert_fusion.3) | copy-start | bytes 589828
  42.3 1.0 copy-start.7
  42.3 1.5 %copy-start.9 = (bf16[768,128]{1,0:T(8,128)(2,1)S(1)}, bf16[768,128]{1,0:T(8,128)(2,1)}, u32[]{:S(2)}) copy-start(bf16[768,128]{1,0:T(8,128)(2,1)} %copy-done.8) | copy-start | bytes 589828
  50.5 31.8 %copy-start.5 = (bf16[128,8,128]{0,2,1:T(8,128)(2,1)S(1)}, bf16[128,8,128]{0,2,1:T(8,128)(2,1)}, u32[]{:S(2)}) copy-start(bf16[128,8,128]{0,2,1:T(8,128)(2,1)} %copy-done.4) | copy-start | bytes 786436
  80.1 1.7 %copy-start.1 = (bf16[4,3072,128]{2,1,0:T(8,128)(2,1)}, bf16[4,3072,128]{2,1,0:T(8,128)(2,1)S(1)}, u32[]{:S(2)}) copy-start(bf16[4,3072,128]{2,1,0:T(8,128)(2,1)S(1)} %get-tuple-element.18) | copy-start | bytes 9437188
